TPU v7x, 256 devices: a whole 4x4x8 slice. The times are simulated.
256 devices in a mesh: pipe: 8 (over y, z_lo), expert: 32 (over z_hi, x, core).
Axes of the slice: x: 4, y: 4, z: 8 (z_hi: 4, z_lo: 2; z = z_hi * 2 + z_lo), core: 2. Of those that a mesh axis runs over, the one named last changes fastest.
Arguments:
- acts: bfloat16 [8, 4096, 3584], P('pipe', 'expert'), may hold values from -6 to 6
- routes: int32 [3, 8, 4096, 8], P(None, 'pipe', 'expert'), may hold values from 0 to 255, all different within a row
- gates: float32 [3, 8, 4096, 8], P(None, 'pipe', 'expert'), may hold values from 0.1 to 1
- norm_gain: float32 [2, 8, 3584], P(None, 'pipe'), may hold values from 0.1 to 1.9
- gate_weight: bfloat16 [2, 8, 3584, 8192], P(None, 'pipe', None, 'expert'), may hold values from -0.09375 to 0.09375
- up_weight: bfloat16 [2, 8, 3584, 8192], P(None, 'pipe', None, 'expert'), may hold values from -0.09375 to 0.09375
- down_weight: bfloat16 [2, 8, 8192, 3584], P(None, 'pipe', 'expert'), may hold values from -0.125 to 0.125
Outputs:
- acts_out: bfloat16 [8, 4096, 3584], P('pipe', 'expert')
Inputs may be any that keep to these rules, and one draw needn't show every extreme that they name: `routes`: each token names 8 different expert ids; only ids below 4 act in this window.
All inputs are finite; a program needn't handle non-finite values.
Results may differ from a plain program's by a relative error of at most 0.0034.
Values may be sent and summed in bfloat16 or wider, within the bound.
A program may use at most 64 MiB of HBM per device.

v0:
```python
import jax
import jax.numpy as jnp
from jax import lax
from jax.sharding import PartitionSpec as P

SLICES = 8
CAP = 8


epsilon = 1e-06


def from_behind(shard, axis, by):
    size = lax.axis_size(axis)
    return lax.ppermute(shard, axis, [(i, (i + by) % size) for i in range(size)])


def normalize(tokens_in, gain_row):
    x_float = tokens_in.astype(jnp.float32)
    inverse = lax.rsqrt(jnp.mean(x_float * x_float, axis=-1, keepdims=True) + epsilon)
    return (x_float, (x_float * inverse * gain_row).astype(jnp.bfloat16))


def expert_rows(incoming, w_gate, w_up, w_down):
    sources, count, width = incoming.shape
    flat = incoming.reshape(sources * count, width)
    gate_part = jnp.dot(flat, w_gate, preferred_element_type=jnp.float32)
    up_part = jnp.dot(flat, w_up, preferred_element_type=jnp.float32)
    hidden = (jax.nn.silu(gate_part) * up_part).astype(jnp.bfloat16)
    partial_value = jnp.dot(hidden, w_down, preferred_element_type=jnp.float32).astype(jnp.bfloat16)
    return partial_value.reshape(sources, count, width)


def moe_layer(tokens_in, route_ids, gate_values, gain_row, w_gate, w_up, w_down):
    x_float, normed = normalize(tokens_in, gain_row)
    tokens_here, width = normed.shape
    devices = lax.axis_size("expert")
    in_flight = devices // SLICES
    expert_ids = jnp.arange(in_flight, dtype=jnp.int32)
    slot_ids = jnp.arange(CAP, dtype=jnp.int32)
    matches = route_ids[:, :, None] == expert_ids[None, None, :]
    taken_count = jnp.sum(matches.astype(jnp.int32), axis=1)
    weight = jnp.sum(jnp.where(matches, gate_values[:, :, None], jnp.float32(0.0)), axis=1)
    before = jnp.cumsum(taken_count, axis=0) - taken_count
    kept_mask = taken_count * (before < CAP).astype(jnp.int32)
    placing = (
        kept_mask[:, :, None] * (before[:, :, None] == slot_ids[None, None, :]).astype(jnp.int32)
    ).astype(jnp.float32)
    dispatch_table = placing.reshape(tokens_here, in_flight * CAP).astype(jnp.bfloat16)
    packed = jnp.einsum(
        "tc,td->cd", dispatch_table, normed, preferred_element_type=jnp.float32
    ).astype(jnp.bfloat16)
    mixing = (placing * weight[:, :, None]).reshape(tokens_here, in_flight * CAP)
    outgoing = jnp.broadcast_to(
        packed.reshape(in_flight, 1, CAP, width), (in_flight, SLICES, CAP, width)
    ).reshape(devices, CAP, width)
    returned_rows = lax.all_to_all(
        expert_rows(
            lax.all_to_all(outgoing, "expert", split_axis=0, concat_axis=0, tiled=True),
            w_gate,
            w_up,
            w_down,
        ),
        "expert",
        split_axis=0,
        concat_axis=0,
        tiled=True,
    )
    expert_out = (
        jnp.sum(returned_rows.reshape(in_flight, SLICES, CAP, width).astype(jnp.float32), axis=1)
        .astype(jnp.bfloat16)
        .reshape(in_flight * CAP, width)
    )
    output = x_float + jnp.dot(
        mixing, expert_out.astype(jnp.float32), preferred_element_type=jnp.float32
    )
    return output.astype(jnp.bfloat16)


def per_device(acts, routes, gates, norm_gain, gate_weight, up_weight, down_weight):
    section_index = lax.axis_index("pipe")
    current = acts[0]
    for moment in range(routes.shape[0]):
        second = (section_index < moment).astype(jnp.int32)

        def select(stacked):
            return lax.dynamic_index_in_dim(stacked, second, 0, keepdims=False)[0]

        current = moe_layer(
            current,
            routes[moment, 0],
            gates[moment, 0],
            select(norm_gain),
            select(gate_weight),
            select(up_weight),
            select(down_weight),
        )
        current = from_behind(current, "pipe", 1)
    return current[None]


def solution(mesh):
    return jax.shard_map(
        per_device,
        mesh=mesh,
        in_specs=(
            P("pipe", "expert", None),
            P(None, "pipe", "expert", None),
            P(None, "pipe", "expert", None),
            P(None, "pipe", None),
            P(None, "pipe", None, "expert"),
            P(None, "pipe", None, "expert"),
            P(None, "pipe", "expert", None),
        ),
        out_specs=P("pipe", "expert", None),
        check_vma=False,
    )
```

profile of v0, /device:TPU:32, one launch (start us, length us, event | category | flops | bytes accessed | tf_op | source)
XLA Modules:
  0.0 406.0 jit_solution(12886075482636263259)
XLA Ops:
  0.0 1.4 fusion.13
  1.5 0.7 slice_bitcast_fusion.1
  2.6 0.9 dynamic-slice_reduce_fusion
  3.5 1.6 fusion.9
  5.3 56.3 %all_to_all.30 = bf16[32,8,3584]{2,1,0:T(8,128)(2,1)S(1)} all-to-all(bf16[32,8,3584]{2,1,0:T(8,128)(2,1)S(1)} %bitcast.171), channel_id=1, replica_groups=mesh['pipe'=8,'expert'=32] {'expert'}, dimensions={0} | all-to-all | bytes 3670016 | tf_op jit(solution)/shard_map/all_to_all | solution.py:59
  61.5 0.6 fusion.39
  62.2 5.4 %fusion = bf16[32,8,3584]{2,1,0:T(8,128)(2,1)} fusion(bf16[2,1,256,3584]{3,2,1,0:T(8,128)(2,1)} %param.13, s32[]{:T(128)S(6)} %select_n.32, bf16[2,1,3584,256]{3,2,1,0:T(8,128)(2,1)} %param.12, bf16[32,8,3584]{2,1,0:T(8,128)(2,1)S(1)} %all_to_all.30, f32[256,256]{1,0:T(8,128)S(1)} %fusion.39), kind=kOutput, calls=%fused_computation.3 | convolution fusion | flops 940834816 | bytes 7603200 | tf_op jit(solution)/shard_map/dot_general | solution.py:30
  67.6 4.7 %all-to-all-start.1 = ((bf16[32,8,3584]{2,1,0:T(8,128)(2,1)}), bf16[32,8,3584]{2,1,0:T(8,128)(2,1)S(1)}, u32[]{:S(2)}, u32[]{:S(2)}) async-start(bf16[32,8,3584]{2,1,0:T(8,128)(2,1)} %fusion), calls=%async_computation.1 | async-start | bytes 3670016 | tf_op jit(solution)/shard_map/all_to_all | solution.py:57
  72.4 37.3 %all-to-all-done.1 = bf16[32,8,3584]{2,1,0:T(8,128)(2,1)S(1)} async-done(((bf16[32,8,3584]{2,1,0:T(8,128)(2,1)}), bf16[32,8,3584]{2,1,0:T(8,128)(2,1)S(1)}, u32[]{:S(2)}, u32[]{:S(2)}) %all-to-all-start.1) | async-done | bytes 1835040 | tf_op jit(solution)/shard_map/all_to_all | solution.py:57
  110.4 10.0 %collective-permute-start = (bf16[128,3584]{1,0:T(8,128)(2,1)S(1)}, bf16[128,3584]{1,0:T(8,128)(2,1)S(1)}, u32[]{:S(2)}, u32[]{:S(2)}) collective-permute-start(bf16[128,3584]{1,0:T(8,128)(2,1)S(1)} %fusion.8), channel_id=1, source_target_pairs={{0,32},{32,64},{64,96},{96,128},{128,160},{160,192},{192,224},{224... | collective-permute-start | bytes 2752520 | tf_op jit(solution)/shard_map/ppermute | solution.py:15
  120.9 20.2 %collective-permute-done = bf16[128,3584]{1,0:T(8,128)(2,1)S(1)} collective-permute-done((bf16[128,3584]{1,0:T(8,128)(2,1)S(1)}, bf16[128,3584]{1,0:T(8,128)(2,1)S(1)}, u32[]{:S(2)}, u32[]{:S(2)}) %collective-permute-start) | collective-permute-done | bytes 917536 | tf_op jit(solution)/shard_map/ppermute | solution.py:15
  142.0 41.5 %all_to_all.31 = bf16[32,8,3584]{2,1,0:T(8,128)(2,1)S(1)} all-to-all(bf16[32,8,3584]{2,1,0:T(8,128)(2,1)S(1)} %bitcast.172), channel_id=1, replica_groups=mesh['pipe'=8,'expert'=32] {'expert'}, dimensions={0} | all-to-all | bytes 3670016 | tf_op jit(solution)/shard_map/all_to_all | solution.py:59
  184.1 5.4 %fusion.1 = bf16[32,8,3584]{2,1,0:T(8,128)(2,1)} fusion(bf16[2,1,256,3584]{3,2,1,0:T(8,128)(2,1)} %param.13, s32[]{:T(128)S(6)} %select_n.34, bf16[2,1,3584,256]{3,2,1,0:T(8,128)(2,1)} %param.12, bf16[32,8,3584]{2,1,0:T(8,128)(2,1)S(1)} %all_to_all.31, f32[256,256]{1,0:T(8,128)S(1)} %fusion.32), kind=kOutput, calls=%fused_computation.4 | convolution fusion | flops 940834816 | bytes 7603200 | tf_op jit(solution)/shard_map/dot_general | solution.py:30
  189.6 14.6 %all-to-all-start.3 = ((bf16[32,8,3584]{2,1,0:T(8,128)(2,1)}), bf16[32,8,3584]{2,1,0:T(8,128)(2,1)S(1)}, u32[]{:S(2)}, u32[]{:S(2)}) async-start(bf16[32,8,3584]{2,1,0:T(8,128)(2,1)} %fusion.1), calls=%async_computation.3 | async-start | bytes 3670016 | tf_op jit(solution)/shard_map/all_to_all | solution.py:57
  204.2 37.3 %all-to-all-done.3 = bf16[32,8,3584]{2,1,0:T(8,128)(2,1)S(1)} async-done(((bf16[32,8,3584]{2,1,0:T(8,128)(2,1)}), bf16[32,8,3584]{2,1,0:T(8,128)(2,1)S(1)}, u32[]{:S(2)}, u32[]{:S(2)}) %all-to-all-start.3) | async-done | bytes 1835040 | tf_op jit(solution)/shard_map/all_to_all | solution.py:57
  242.2 11.1 %collective-permute-start.1 = (bf16[128,3584]{1,0:T(8,128)(2,1)S(1)}, bf16[128,3584]{1,0:T(8,128)(2,1)S(1)}, u32[]{:S(2)}, u32[]{:S(2)}) collective-permute-start(bf16[128,3584]{1,0:T(8,128)(2,1)S(1)} %fusion.7), channel_id=1, source_target_pairs={{0,32},{32,64},{64,96},{96,128},{128,160},{160,192},{192,224},{224... | collective-permute-start | bytes 2752520 | tf_op jit(solution)/shard_map/ppermute | solution.py:15
  253.6 19.8 %collective-permute-done.1 = bf16[128,3584]{1,0:T(8,128)(2,1)S(1)} collective-permute-done((bf16[128,3584]{1,0:T(8,128)(2,1)S(1)}, bf16[128,3584]{1,0:T(8,128)(2,1)S(1)}, u32[]{:S(2)}, u32[]{:S(2)}) %collective-permute-start.1) | collective-permute-done | bytes 917536 | tf_op jit(solution)/shard_map/ppermute | solution.py:15
  274.3 41.1 %all_to_all.32 = bf16[32,8,3584]{2,1,0:T(8,128)(2,1)S(1)} all-to-all(bf16[32,8,3584]{2,1,0:T(8,128)(2,1)S(1)} %bitcast.173), channel_id=1, replica_groups=mesh['pipe'=8,'expert'=32] {'expert'}, dimensions={0} | all-to-all | bytes 3670016 | tf_op jit(solution)/shard_map/all_to_all | solution.py:59
  316.0 5.4 %fusion.2 = bf16[32,8,3584]{2,1,0:T(8,128)(2,1)} fusion(bf16[2,1,256,3584]{3,2,1,0:T(8,128)(2,1)} %param.13, s32[]{:T(128)S(6)} %select_n.36, bf16[2,1,3584,256]{3,2,1,0:T(8,128)(2,1)} %param.12, bf16[32,8,3584]{2,1,0:T(8,128)(2,1)S(1)} %all_to_all.32, f32[256,256]{1,0:T(8,128)S(1)} %fusion.25), kind=kOutput, calls=%fused_computation.5 | convolution fusion | flops 940834816 | bytes 7603200 | tf_op jit(solution)/shard_map/dot_general | solution.py:30
  321.5 14.6 %all-to-all-start.5 = ((bf16[32,8,3584]{2,1,0:T(8,128)(2,1)}), bf16[32,8,3584]{2,1,0:T(8,128)(2,1)S(1)}, u32[]{:S(2)}, u32[]{:S(2)}) async-start(bf16[32,8,3584]{2,1,0:T(8,128)(2,1)} %fusion.2), calls=%async_computation.5 | async-start | bytes 3670016 | tf_op jit(solution)/shard_map/all_to_all | solution.py:57
  336.1 37.3 %all-to-all-done.5 = bf16[32,8,3584]{2,1,0:T(8,128)(2,1)S(1)} async-done(((bf16[32,8,3584]{2,1,0:T(8,128)(2,1)}), bf16[32,8,3584]{2,1,0:T(8,128)(2,1)S(1)}, u32[]{:S(2)}, u32[]{:S(2)}) %all-to-all-start.5) | async-done | bytes 1835040 | tf_op jit(solution)/shard_map/all_to_all | solution.py:57
  374.0 10.4 %collective-permute-start.2 = (bf16[128,3584]{1,0:T(8,128)(2,1)S(1)}, bf16[128,3584]{1,0:T(8,128)(2,1)S(1)}, u32[]{:S(2)}, u32[]{:S(2)}) collective-permute-start(bf16[128,3584]{1,0:T(8,128)(2,1)S(1)} %fusion.6), channel_id=1, source_target_pairs={{0,32},{32,64},{64,96},{96,128},{128,160},{160,192},{192,224},{224... | collective-permute-start | bytes 2752520 | tf_op jit(solution)/shard_map/ppermute | solution.py:15
  384.4 20.7 %collective-permute-done.2 = bf16[128,3584]{1,0:T(8,128)(2,1)S(1)} collective-permute-done((bf16[128,3584]{1,0:T(8,128)(2,1)S(1)}, bf16[128,3584]{1,0:T(8,128)(2,1)S(1)}, u32[]{:S(2)}, u32[]{:S(2)}) %collective-permute-start.2) | collective-permute-done | bytes 917536 | tf_op jit(solution)/shard_map/ppermute | solution.py:15
  405.1 0.9 copy.42
  (49 shorter events, 6.5 us)
Async XLA Ops:
  5.3 56.3 %copy-start = (bf16[2,1,3584,256]{3,2,1,0:T(8,128)(2,1)S(1)}, bf16[2,1,3584,256]{3,2,1,0:T(8,128)(2,1)}, u32[]{:S(2)}) copy-start(bf16[2,1,3584,256]{3,2,1,0:T(8,128)(2,1)} %param.11) | copy-start | bytes 11010052
  67.6 4.7 %copy-start.4 = (f32[3,1,128,8]{2,3,1,0:T(8,128)S(1)}, f32[3,1,128,8]{2,3,1,0:T(8,128)}, u32[]{:S(2)}) copy-start(f32[3,1,128,8]{2,3,1,0:T(8,128)} %param.9) | copy-start | bytes 36868
  67.6 42.1 %all-to-all-start.1 = ((bf16[32,8,3584]{2,1,0:T(8,128)(2,1)}), bf16[32,8,3584]{2,1,0:T(8,128)(2,1)S(1)}, u32[]{:S(2)}, u32[]{:S(2)}) async-start(bf16[32,8,3584]{2,1,0:T(8,128)(2,1)} %fusion), calls=%async_computation.1 | async-start | bytes 3670016 | tf_op jit(solution)/shard_map/all_to_all | solution.py:57
  72.3 37.6 %copy-start.3 = (bf16[1,128,3584]{2,1,0:T(8,128)(2,1)S(1)}, bf16[1,128,3584]{2,1,0:T(8,128)(2,1)}, u32[]{:S(2)}) copy-start(bf16[1,128,3584]{2,1,0:T(8,128)(2,1)} %param.7) | copy-start | bytes 2752516
  110.4 30.7 %collective-permute-start = (bf16[128,3584]{1,0:T(8,128)(2,1)S(1)}, bf16[128,3584]{1,0:T(8,128)(2,1)S(1)}, u32[]{:S(2)}, u32[]{:S(2)}) collective-permute-start(bf16[128,3584]{1,0:T(8,128)(2,1)S(1)} %fusion.8), channel_id=1, source_target_pairs={{0,32},{32,64},{64,96},{96,128},{128,160},{160,192},{192,224},{224... | collective-permute-start | bytes 2752520 | tf_op jit(solution)/shard_map/ppermute | solution.py:15
  141.9 41.6 %copy-start.1 = (bf16[2,1,3584,256]{3,2,1,0:T(8,128)(2,1)S(1)}, bf16[2,1,3584,256]{3,2,1,0:T(8,128)(2,1)}, u32[]{:S(2)}) copy-start(bf16[2,1,3584,256]{3,2,1,0:T(8,128)(2,1)} %param.11) | copy-start | bytes 11010052
  189.6 51.9 %all-to-all-start.3 = ((bf16[32,8,3584]{2,1,0:T(8,128)(2,1)}), bf16[32,8,3584]{2,1,0:T(8,128)(2,1)S(1)}, u32[]{:S(2)}, u32[]{:S(2)}) async-start(bf16[32,8,3584]{2,1,0:T(8,128)(2,1)} %fusion.1), calls=%async_computation.3 | async-start | bytes 3670016 | tf_op jit(solution)/shard_map/all_to_all | solution.py:57
  242.2 31.2 %collective-permute-start.1 = (bf16[128,3584]{1,0:T(8,128)(2,1)S(1)}, bf16[128,3584]{1,0:T(8,128)(2,1)S(1)}, u32[]{:S(2)}, u32[]{:S(2)}) collective-permute-start(bf16[128,3584]{1,0:T(8,128)(2,1)S(1)} %fusion.7), channel_id=1, source_target_pairs={{0,32},{32,64},{64,96},{96,128},{128,160},{160,192},{192,224},{224... | collective-permute-start | bytes 2752520 | tf_op jit(solution)/shard_map/ppermute | solution.py:15
  274.3 41.1 %copy-start.2 = (bf16[2,1,3584,256]{3,2,1,0:T(8,128)(2,1)S(1)}, bf16[2,1,3584,256]{3,2,1,0:T(8,128)(2,1)}, u32[]{:S(2)}) copy-start(bf16[2,1,3584,256]{3,2,1,0:T(8,128)(2,1)} %param.11) | copy-start | bytes 11010052
  321.5 51.9 %all-to-all-start.5 = ((bf16[32,8,3584]{2,1,0:T(8,128)(2,1)}), bf16[32,8,3584]{2,1,0:T(8,128)(2,1)S(1)}, u32[]{:S(2)}, u32[]{:S(2)}) async-start(bf16[32,8,3584]{2,1,0:T(8,128)(2,1)} %fusion.2), calls=%async_computation.5 | async-start | bytes 3670016 | tf_op jit(solution)/shard_map/all_to_all | solution.py:57
  374.0 31.0 %collective-permute-start.2 = (bf16[128,3584]{1,0:T(8,128)(2,1)S(1)}, bf16[128,3584]{1,0:T(8,128)(2,1)S(1)}, u32[]{:S(2)}, u32[]{:S(2)}) collective-permute-start(bf16[128,3584]{1,0:T(8,128)(2,1)S(1)} %fusion.6), channel_id=1, source_target_pairs={{0,32},{32,64},{64,96},{96,128},{128,160},{160,192},{192,224},{224... | collective-permute-start | bytes 2752520 | tf_op jit(solution)/shard_map/ppermute | solution.py:15
where the time goes:
time: 410 us; the launch traced here: 406 us
  waiting for transfers between devices  173 us (42%)
  blocking collectives  139 us (34%)
  starting transfers between devices  65.3 us (16%)
  matrix products  22 us (5%)
    all_to_all x3, blocking collectives, moe_layer(): lax.all_to_all(outgoing, 'expert', split_axis=0, concat_axis=0, tiled=True)  139 us
    all_to_all x3, waiting for transfers between devices, moe_layer(): lax.all_to_all(expert_rows(lax.all_to_all(outgoing, 'expert', split_axis=...  112 us
    ppermute x3, waiting for transfers between devices, from_behind(): lax.ppermute(shard, axis, [(i, (i + by) % size) for i in range(size)])  60.7 us
    all_to_all x3, starting transfers between devices, moe_layer(): lax.all_to_all(expert_rows(lax.all_to_all(outgoing, 'expert', split_axis=...  33.9 us
    ppermute x3, starting transfers between devices, from_behind(): lax.ppermute(shard, axis, [(i, (i + by) % size) for i in range(size)])  31.4 us
    dot_general x3, matrix products, expert_rows(): jnp.dot(hidden, w_down, preferred_element_type=jnp.float32)  16.2 us
  transfers between devices with their start and end apart: 6, of which 6 were waited for; matrix products, arithmetic and copies ran while one was open for 0% of the time, Pallas kernels for 0%

commit v1 on v0

v1 whole, which is shorter than its diff:
```python
import jax
import jax.numpy as jnp
from jax import lax
from jax.experimental import pallas as pl
from jax.experimental.pallas import tpu as pltpu
from jax.sharding import PartitionSpec as P

CAP = 8
EXPERTS = 4
NP = 8
NZ = 4
NX = 4
D = 3584
H = 2
DH = D // H
TOK = 128
HID = 256
TICKS = 3
DORD = (0, 1, 2, 3)
CROSS = (0, 0, 0)
DIRECT = 1
SLOTS = EXPERTS * CAP
epsilon = 1e-06
F32 = jnp.float32
BF16 = jnp.bfloat16
MESH = pl.DeviceIdType.MESH
NT = (((1,), (1,)), ((), ()))


def kernel(
    acts, routes, gates, gain, gw, uw, dw, out,
    x0, x1, xs, xs2, x3, ga, gb, gc, mt, tab_a, tab_b, tab_c,
    wg, wu, wd, ag, zs, rw, pre, acc, hid, pf, s1, s1r, s2, s2r, plain, plainr, eob, ret,
    in_sem, w_sem, wp_ssem, wp_rsem, t_ssem, t_rsem, b_ssem, b_rsem,
    x_ssem, z_ssem, z_rsem, xl_rsem, xr_rsem, rl_rsem, rr_rsem, a_rsem, c_rsem, d_rsem, e_rsem, p_rsem, q_rsem, v_rsem, u_rsem, r_rsem,
):
    p = lax.axis_index("pipe")
    q = lax.axis_index("expert")
    z = q // 8
    x = lax.rem(q // 2, NX)
    c = lax.rem(q, 2)
    odd = lax.rem(p, 2)

    def dev(dp, zz, xx, cc):
        return {"pipe": lax.rem(p + dp, NP), "expert": zz * 8 + xx * 2 + cc}

    def same(dp):
        return dev(dp, z, x, c)

    def other(t):
        return 1 - c if CROSS[t] else c

    near = NZ - DIRECT
    partner = dev(0, z, x, 1 - c)
    right = dev(0, z, lax.rem(x + 1, NX), c)
    left = dev(0, z, lax.rem(x + 3, NX), c)
    across = dev(0, z, lax.rem(x + 2, NX), c)

    def rc(src, dst, ss, rs, to):
        return pltpu.make_async_remote_copy(
            src_ref=src, dst_ref=dst, send_sem=ss, recv_sem=rs, device_id=to, device_id_type=MESH
        )

    def send(src, dst, ss, rs, to):
        rc(src, dst, ss, rs, to).start()

    def got(ref, sem):
        rc(ref, ref, sem, sem, right).wait_recv()

    def sent(ref, sem):
        rc(ref, ref, sem, sem, right).wait_send()

    def each(body):
        lax.fori_loop(0, H, lambda h, carry: (body(h), carry)[1], 0)

    def cols(h):
        return pl.ds(pl.multiple_of(h * DH, 128), DH)

    def z_even(offset):
        return lax.rem(z + offset, NZ)

    def z_next(k):
        if k == 0 or k == 3:
            return lax.rem(z + (0, 0, 0, 2)[k], NZ)
        return lax.rem(z + (2 * odd + 3 if k == 1 else 5 - 2 * odd), NZ)

    def dst_z(t, k):
        return z_next(k) if t == 1 else z_even((0, 1, 3, 2)[k])

    def home_z(t, k):
        return z_next(k) if t == 1 else z_even((0, 3, 1, 2)[k])

    barrier = pltpu.get_barrier_semaphore()
    flows = {(dp, cross) for t, pair in enumerate(((0, 2), (7, 1), (0, 1))) for dp in pair for cross in (CROSS[t],)}
    flows |= {((NP - dp) % NP, cross) for dp, cross in flows}
    places = {(dp, dz, cross) for dp, cross in flows for dz in range(NZ)} | {(dp, 0, 0) for dp in (1, 2, 6, 7)}
    places = sorted(places - {(0, 0, 0)} | {(0, 0, 1)})
    peers = [right, left, across] + [dev(dp, lax.rem(z + dz, NZ), x, 1 - c if cross else c) for dp, dz, cross in places]
    for peer in peers:
        pl.semaphore_signal(barrier, inc=1, device_id=peer, device_id_type=MESH)

    v1 = (8 - p) // 8
    v2 = (9 - p) // 8

    each(lambda h: pltpu.make_async_copy(acts.at[0, :, cols(h)], x0.at[h], in_sem.at[0]).start())
    pltpu.make_async_copy(gain.at[0], ga, in_sem.at[1]).start()
    pltpu.make_async_copy(gain.at[v2], gc, in_sem.at[2]).start()
    mats = ((gw, wg), (uw, wu), (dw, wd))
    earlier = (
        lax.broadcasted_iota(jnp.int32, (TOK, TOK), 0) < lax.broadcasted_iota(jnp.int32, (TOK, TOK), 1)
    ).astype(F32).astype(BF16)
    slot = lax.broadcasted_iota(jnp.int32, (CAP, TOK), 0).astype(F32)

    def table(t, carry):
        ids, values = routes[t, 0], gates[t, 0]
        taken, weight = [], []
        for e in range(EXPERTS):
            match = ids == e
            taken.append(jnp.sum(jnp.where(match, F32(1.0), F32(0.0)), axis=0, keepdims=True))
            weight.append(jnp.sum(jnp.where(match, values, F32(0.0)), axis=0, keepdims=True))
        four = jnp.concatenate(taken + [jnp.zeros((4, TOK), F32)], axis=0)
        before = jnp.dot(four.astype(BF16), earlier, preferred_element_type=F32)
        for e in range(EXPERTS):
            here = (before[e:e + 1] == slot) & (taken[e] > 0.5)
            mt[t, e * CAP:(e + 1) * CAP] = jnp.where(here, weight[e], F32(0.0))
        return carry

    lax.fori_loop(0, TICKS, table, 0)

    def chosen(tab):
        return (tab > 0).astype(F32).astype(BF16)

    def halves(tab):
        high = tab.astype(BF16).astype(F32)
        return high, tab - high

    def mixer(tab):
        high, low = halves(tab)
        return jnp.concatenate([high, low, jnp.zeros((64, TOK), F32)], axis=0).T.astype(BF16)

    def returned(t, h):
        return ret[t, :, h].astype(F32).reshape(SLOTS, DH)

    def dispatch(t, gref, dp, local):
        total = jnp.zeros((SLOTS, 1), F32)
        for h in range(H):
            total += jnp.sum(rw[h] * rw[h], axis=-1, keepdims=True)
        inverse = lax.rsqrt(total / D + epsilon)

        def scale(h):
            rows = (rw[h] * inverse * gref[:, cols(h)]).reshape(EXPERTS, CAP, DH).astype(BF16)
            zs[t, :, h] = rows

        each(scale)

        def go():
            for k in DORD:
                if not (local and k == 0):
                    zz = dst_z(t, k)
                    send(zs.at[t, zz], ag.at[t, :, 0, k], z_ssem.at[t], z_rsem.at[t, k], dev(dp, zz, x, other(t)))
            if local:
                for h in range(H):
                    ag[t, h, 0, 0] = zs[t, z, h]
        return go

    def expert(t, sel, local, home, before_first, after_first, before_end):
        def first(k):
            if not (local and k == 0):
                got(ag.at[t, :, 0, k], z_rsem.at[t, k])
            if k >= near:
                send(ag.at[t, :, 0, k], ag.at[t, :, 3, k], x_ssem.at[11], v_rsem.at[t % 2, k], across)
            send(ag.at[t, :, 0, k], ag.at[t, :, 1, k], x_ssem.at[0], xl_rsem.at[t % 2, k], right)
            send(ag.at[t, :, 0, k], ag.at[t, :, 2, k], x_ssem.at[1], xr_rsem.at[t % 2, k], left)

        def relay(k):
            got(ag.at[t, :, 1, k], xl_rsem.at[t % 2, k])
            if k < near:
                send(ag.at[t, 0, 1, k], ag.at[t, 0, 3, k], x_ssem.at[2], rl_rsem.at[t % 2], right)
            got(ag.at[t, :, 2, k], xr_rsem.at[t % 2, k])
            if k < near:
                send(ag.at[t, 1, 2, k], ag.at[t, 1, 3, k], x_ssem.at[3], rr_rsem.at[t % 2], left)
            else:
                got(ag.at[t, :, 3, k], v_rsem.at[t % 2, k])

        before_first()
        first(0)
        after_first()
        first(1)
        first(2)
        relay(0)
        first(3)
        relay(1)
        relay(2)
        relay(3)

        if t == 0:
            for i, (src, dst) in enumerate(mats[:2]):
                pltpu.make_async_copy(src.at[0, 0], dst.at[0, c], w_sem.at[0, i]).wait()
                got(dst.at[0, 1 - c], wp_rsem.at[0, i])
        if t == 1:
            @pl.when(p < 2)
            def _():
                for i, (src, dst) in enumerate(mats):
                    pltpu.make_async_copy(src.at[1, 0], dst.at[1, c], w_sem.at[1, i]).wait()
                    got(dst.at[1, 1 - c], wp_rsem.at[1, i])

        for h in range(H):
            if near:
                got(ag.at[t, h, 3, 0:near], (rl_rsem if h == 0 else rr_rsem).at[t % 2])
            rows = ag[t, h].astype(F32).reshape(TOK, DH).astype(BF16)
            at = pl.ds(h * DH, DH)
            for i in range(2):
                g = jnp.dot(rows, wg[sel, i, at, :], preferred_element_type=F32)
                u = jnp.dot(rows, wu[sel, i, at, :], preferred_element_type=F32)
                if h == 0:
                    acc[i] = g
                    acc[2 + i] = u
                else:
                    g = acc[i] + g
                    u = acc[2 + i] + u
                    hid[i] = (g / (1.0 + jnp.exp(-g)) * u).astype(BF16)
        if t == 0:
            pltpu.make_async_copy(dw.at[0, 0], wd.at[0, c], w_sem.at[0, 2]).wait()
            got(wd.at[0, 1 - c], wp_rsem.at[0, 2])

        for h in range(H):
            part = jnp.dot(hid[0], wd[sel, 0, :, h * DH:(h + 1) * DH], preferred_element_type=F32)
            part += jnp.dot(hid[1], wd[sel, 1, :, h * DH:(h + 1) * DH], preferred_element_type=F32)
            part = part.reshape(NX, NZ, CAP, DH)
            s1[t, h] = part[3].astype(BF16)
            pf[h] = part[0:3]
            plain[t, h] = part[1 + h].astype(BF16)
            for k in range(near, NZ):
                s2[t, h, k] = part[2 - h, k].astype(BF16)
            ahead, behind = (right, left) if h == 0 else (left, right)
            d_sem, p_sem = (d_rsem, p_rsem) if h == 0 else (e_rsem, q_rsem)
            for k in reversed(range(near, NZ)):
                send(s1.at[t, h, k], s1r.at[t, h, k], x_ssem.at[12], u_rsem.at[t % 2, h, k], across)
                send(s2.at[t, h, k], s2r.at[t, h, k], x_ssem.at[6 + h], d_sem.at[t % 2, k], ahead)
                send(plain.at[t, h, k], plainr.at[t, h, k], x_ssem.at[9 + h], p_sem.at[t % 2, k], behind)
            for k in reversed(range(near)):
                send(s1.at[t, h, k], s1r.at[t, h, k], x_ssem.at[4 + h], (a_rsem if h == 0 else c_rsem).at[t % 2, k], ahead)
        if near:
            at = slice(0, near)
            send(plain.at[t, 1, at], plainr.at[t, 1, at], x_ssem.at[10], q_rsem.at[t % 2, 0], right)
            send(plain.at[t, 0, at], plainr.at[t, 0, at], x_ssem.at[9], p_rsem.at[t % 2, 0], left)

        def middle(k):
            got(s1r.at[t, 0, k], a_rsem.at[t % 2, k])
            s2[t, 0, k] = (pf[0, 2, k] + s1r[t, 0, k].astype(F32)).astype(BF16)
            send(s2.at[t, 0, k], s2r.at[t, 0, k], x_ssem.at[6], d_rsem.at[t % 2, k], right)
            got(s1r.at[t, 1, k], c_rsem.at[t % 2, k])
            s2[t, 1, k] = (pf[1, 1, k] + s1r[t, 1, k].astype(F32)).astype(BF16)
            send(s2.at[t, 1, k], s2r.at[t, 1, k], x_ssem.at[7], e_rsem.at[t % 2, k], left)

        def final(k):
            if k >= near:
                for h in range(H):
                    got(s1r.at[t, h, k], u_rsem.at[t % 2, h, k])
                    got(plainr.at[t, h, k], (p_rsem if h == 0 else q_rsem).at[t % 2, k])
            got(s2r.at[t, 0, k], d_rsem.at[t % 2, k])
            got(s2r.at[t, 1, k], e_rsem.at[t % 2, k])
            for h in range(H):
                total = pf[h, 0, k] + s2r[t, h, k].astype(F32) + plainr[t, h, k].astype(F32)
                if k >= near:
                    total += s1r[t, h, k].astype(F32)
                eob[t, k, h] = total.astype(BF16)
            send(eob.at[t, k], ret.at[t, z], x_ssem.at[8], r_rsem.at[t], dev(home, home_z(t, k), x, other(t)))

        for k in reversed(range(near)):
            middle(k)
        for k in reversed(range(near, NZ)):
            final(k)
        if near:
            got(plainr.at[t, 0, 0:near], p_rsem.at[t % 2, 0])
            got(plainr.at[t, 1, 0:near], q_rsem.at[t % 2, 0])
        for k in reversed(range(near)):
            final(k)
        before_end()
        got(ret.at[t], r_rsem.at[t])

    def experts_sent():
        sent(ag.at[:, :, 0], x_ssem.at[0])
        sent(ag.at[:, :, 0], x_ssem.at[1])
        if near:
            sent(ag.at[:, 0, 1, 0:near], x_ssem.at[2])
            sent(ag.at[:, 1, 2, 0:near], x_ssem.at[3])
            sent(s1.at[:, 0, 0:near], x_ssem.at[4])
            sent(s1.at[:, 1, 0:near], x_ssem.at[5])
        if near < NZ:
            sent(ag.at[:, :, 3, near:], x_ssem.at[11])
            sent(s1.at[:, :, near:], x_ssem.at[12])
        sent(s2.at[:, 0], x_ssem.at[6])
        sent(s2.at[:, 1], x_ssem.at[7])
        sent(eob, x_ssem.at[8])
        sent(plain.at[:, 0], x_ssem.at[9])
        sent(plain.at[:, 1], x_ssem.at[10])

    def combine(t, xref, mix, h):
        rows = returned(t, h)
        rows = jnp.concatenate([rows, rows, jnp.zeros((64, DH), F32)], axis=0).astype(BF16)
        return xref[h].astype(F32) + jnp.dot(mix, rows, preferred_element_type=F32)

    def prepare(tab, xref):
        pick = chosen(tab)

        def one(h):
            pre[h] = jnp.dot(pick, xref[h], preferred_element_type=F32)

        each(one)

    def choose_rows(t, tab, tab_next):
        pick = chosen(tab_next)
        high, low = halves(tab)
        high = lax.dot_general(pick, high.astype(BF16), NT, preferred_element_type=F32)
        low = lax.dot_general(pick, low.astype(BF16), NT, preferred_element_type=F32)
        cross = jnp.concatenate([high, low], axis=0).astype(BF16)

        def one(h):
            added = jnp.dot(cross, returned(t, h).astype(BF16), preferred_element_type=F32)
            value = pre[h] + (added[0:SLOTS] + added[SLOTS:])
            rw[h] = value.astype(BF16).astype(F32)

        each(one)

    pltpu.make_async_copy(x0, x0, in_sem.at[0]).wait()
    pltpu.make_async_copy(gain.at[0], ga, in_sem.at[1]).wait()
    pltpu.make_async_copy(gain.at[v2], gc, in_sem.at[2]).wait()
    pick0 = chosen(mt[0])

    def gather(h):
        rw[h] = jnp.dot(pick0, x0[h], preferred_element_type=F32)

    for i, (src, dst) in enumerate(mats):
        pltpu.make_async_copy(src.at[0, 0], dst.at[0, c], w_sem.at[0, i]).start()
    each(gather)
    go = dispatch(0, ga, 0, True)
    pl.semaphore_wait(barrier, len(peers))
    for i, (src, dst) in enumerate(mats):
        send(src.at[0, 0], dst.at[0, c], wp_ssem.at[0, i], wp_rsem.at[0, i], partner)
    go()

    def background():
        send(mt.at[0], tab_a, t_ssem.at[0], t_rsem.at[0], same(2))
        send(mt.at[1], tab_b, t_ssem.at[1], t_rsem.at[1], same(1))
        send(mt.at[2], tab_c, t_ssem.at[2], t_rsem.at[2], same(1))
        send(gain.at[v1], gb, t_ssem.at[3], t_rsem.at[3], same(1))
        each(lambda h: send(x0.at[h], x1.at[h], b_ssem.at[0], b_rsem.at[0], same(2)))

        @pl.when(p < 2)
        def _():
            for i, (src, dst) in enumerate(mats):
                pltpu.make_async_copy(src.at[1, 0], dst.at[1, c], w_sem.at[1, i]).start()
                send(src.at[1, 0], dst.at[1, c], wp_ssem.at[1, i], wp_rsem.at[1, i], partner)

    def ready1():
        got(tab_a, t_rsem.at[0])
        got(tab_b, t_rsem.at[1])
        got(gb, t_rsem.at[3])
        got(x1, b_rsem.at[0])
        prepare(tab_b[...], x1)

    def nothing():
        pass

    expert(0, 0, True, 2, nothing, background, ready1)

    choose_rows(0, tab_a[...], tab_b[...])
    dispatch(1, gb, 7, False)()

    def update1():
        mix = mixer(tab_a[...])

        def one(h):
            xs[h] = combine(0, x1, mix, h).astype(BF16)

        each(one)

    expert(1, v1, False, 1, update1, nothing, lambda: prepare(mt[2], xs))

    choose_rows(1, tab_b[...], mt[2])
    dispatch(2, gc, 0, not CROSS[2])()

    def update2():
        mix = mixer(tab_b[...])

        def one(h):
            xs2[h] = combine(1, xs, mix, h).astype(BF16)
            send(xs2.at[h], x3.at[h], b_ssem.at[1], b_rsem.at[1], same(1))

        each(one)

    def ready3():
        got(tab_c, t_rsem.at[2])
        got(x3, b_rsem.at[1])

    expert(2, v2, not CROSS[2], 1, nothing, update2, ready3)
    mix_c = mixer(tab_c[...])

    def finish(h):
        out[0, :, cols(h)] = combine(2, x3, mix_c, h).astype(BF16)

    each(finish)

    for t in range(TICKS):
        n = 4 if t == 1 or CROSS[t] else 3
        sent(zs.at[t, 0:n], z_ssem.at[t])
    experts_sent()
    for i, (src, dst) in enumerate(mats):
        sent(src.at[0, 0], wp_ssem.at[0, i])
    for i in range(3):
        sent(mt.at[i], t_ssem.at[i])
    sent(gb, t_ssem.at[3])
    sent(x0, b_ssem.at[0])
    sent(xs2, b_ssem.at[1])

    @pl.when(p < 2)
    def _():
        for i, (src, dst) in enumerate(mats):
            sent(src.at[1, 0], wp_ssem.at[1, i])


def per_device(acts, routes, gates, norm_gain, gate_weight, up_weight, down_weight):
    h = lambda a: pltpu.with_memory_space_constraint(a, pltpu.HBM)
    anyw = pl.BlockSpec(memory_space=pl.ANY)
    vmem = pl.BlockSpec(memory_space=pltpu.VMEM)
    V = pltpu.VMEM
    S = pltpu.SemaphoreType.DMA
    bulk = (H, TOK, DH)
    T = (SLOTS, TOK)
    scratch = [
        V(bulk, BF16), V(bulk, BF16), V(bulk, BF16), V(bulk, BF16), V(bulk, BF16),
        V((1, D), F32), V((1, D), F32), V((1, D), F32),
        V((TICKS, SLOTS, TOK), F32), V(T, F32), V(T, F32), V(T, F32),
        V((2, 2, D, HID), BF16), V((2, 2, D, HID), BF16), V((2, 2, HID, D), BF16),
        V((TICKS, H, NX, NZ, CAP, DH), BF16),
        V((TICKS, EXPERTS, H, CAP, DH), BF16),
        V((H, SLOTS, DH), F32), V((H, SLOTS, DH), F32),
        V((4, TOK, HID), F32),
        V((2, TOK, HID), BF16),
        V((H, 3, NZ, CAP, DH), F32),
        V((TICKS, H, NZ, CAP, DH), BF16), V((TICKS, H, NZ, CAP, DH), BF16),
        V((TICKS, H, NZ, CAP, DH), BF16), V((TICKS, H, NZ, CAP, DH), BF16),
        V((TICKS, H, NZ, CAP, DH), BF16), V((TICKS, H, NZ, CAP, DH), BF16),
        V((TICKS, NZ, H, CAP, DH), BF16),
        V((TICKS, EXPERTS, H, CAP, DH), BF16),
        S((3,)), S((2, 3)), S((2, 3)), S((2, 3)), S((4,)), S((4,)), S((2,)), S((2,)),
    ]
    scratch += [S((13,)), S((TICKS,)), S((TICKS, NZ)), S((2, NZ)), S((2, NZ)), S((2,)), S((2,))]
    scratch += [S((2, NZ))] * 4 + [S((2, NZ))] * 3 + [S((2, 2, NZ)), S((TICKS,))]
    return pl.pallas_call(
        kernel,
        out_shape=jax.ShapeDtypeStruct((1, TOK, D), BF16),
        in_specs=[anyw, vmem, vmem, anyw, anyw, anyw, anyw],
        out_specs=vmem,
        scratch_shapes=scratch,
        compiler_params=pltpu.CompilerParams(
            collective_id=0, has_side_effects=True, vmem_limit_bytes=48 * 1024 * 1024
        ),
    )(h(acts), h(routes.transpose(0, 1, 3, 2)), h(gates.transpose(0, 1, 3, 2)), h(norm_gain), h(gate_weight), h(up_weight), h(down_weight))


def solution(mesh):
    return jax.shard_map(
        per_device,
        mesh=mesh,
        in_specs=(
            P("pipe", "expert", None),
            P(None, "pipe", "expert", None),
            P(None, "pipe", "expert", None),
            P(None, "pipe", None),
            P(None, "pipe", None, "expert"),
            P(None, "pipe", None, "expert"),
            P(None, "pipe", "expert", None),
        ),
        out_specs=P("pipe", "expert", None),
        check_vma=False,
    )
```

time: 410 us -> 103 us (0.25)
  waiting for transfers between devices: 173 us -> 0 us
  blocking collectives: 139 us -> 0 us
  Pallas kernels: 0 us -> 102 us
  starting transfers between devices: 65.3 us -> 0 us
  matrix products: 22 us -> 0 us
    all_to_all x3 -> x0, blocking collectives: 139 us -> none  [moe_layer(): lax.all_to_all(outgoing, 'expert', split_axis=0, concat_axis=0, tiled=True)]
    all_to_all x3 -> x0, waiting for transfers between devices: 112 us -> none  [moe_layer(): lax.all_to_all(expert_rows(lax.all_to_all(outgoing, 'expert', split_axis=...]
    pallas_call x0 -> x1, Pallas kernels: none -> 102 us  [per_device(): pl.pallas_call(kernel, out_shape=jax.ShapeDtypeStruct((1, TOK, D), BF16),...]
    ppermute x3 -> x0, waiting for transfers between devices: 60.7 us -> none  [from_behind(): lax.ppermute(shard, axis, [(i, (i + by) % size) for i in range(size)])]
    all_to_all x3 -> x0, starting transfers between devices: 33.9 us -> none  [moe_layer(): lax.all_to_all(expert_rows(lax.all_to_all(outgoing, 'expert', split_axis=...]
    ppermute x3 -> x0, starting transfers between devices: 31.4 us -> none  [from_behind(): lax.ppermute(shard, axis, [(i, (i + by) % size) for i in range(size)])]
    dot_general x12 -> x0, matrix products: 22 us -> none  [the longest x3 16.2 us: expert_rows(): jnp.dot(hidden, w_down, preferred_element_type=jnp.float32)]
  transfers between devices with their start and end apart: 6 -> 0, of which waited for: 6 -> 0; matrix products, arithmetic and copies ran while one was open for 0% -> 0% of each run, Pallas kernels for 0% -> 0%
where the time goes in v1:
time: 103 us
  Pallas kernels  102 us (99%)
    pallas_call x1, Pallas kernels, per_device(): pl.pallas_call(kernel, out_shape=jax.ShapeDtypeStruct((1, TOK, D), BF16),...  102 us

profile of v1, /device:TPU:32, one launch (start us, length us, event | category | flops | bytes accessed | tf_op | source)
XLA Modules:
  0.0 103.0 jit_solution(5683562306622662250)
XLA Ops:
  0.0 102.1 %shard_map.73 = bf16[1,128,3584]{2,1,0:T(8,128)(2,1)S(1)} custom-call(bf16[1,128,3584]{2,1,0:T(8,128)(2,1)} %acts.1, s32[3,1,8,128]{3,2,1,0:T(8,128)} %bitcast.2, f32[3,1,8,128]{3,2,1,0:T(8,128)} %bitcast.3, f32[2,1,3584]{2,1,0:T(1,128)} %gain.1, bf16[2,1,3584,256]{3,2,1,0:T(8,128)(2,1)} %gw.1, bf16[2,1,3584,256]{3,2,1,0:T(8,128)(2,1)} %uw.1, ...), custom_call_target="tpu_custom_call" | custom-call | tf_op jit(solution)/shard_map/pallas_call | solution.py:451
  102.1 0.9 copy.9

commit v2 on v1

--- a/solution.py
+++ b/solution.py
@@ -6,6 +6,7 @@
 from jax.sharding import PartitionSpec as P
 
 CAP = 8
+TOPK = 8
 EXPERTS = 4
 NP = 8
 NZ = 4
@@ -18,7 +19,10 @@
 TICKS = 3
 DORD = (0, 1, 2, 3)
 CROSS = (0, 0, 0)
-DIRECT = 1
+EARLY = 2
+LATE = 2
+GATHER_NEAR = (3, 2, 3)
+MID = 1
 SLOTS = EXPERTS * CAP
 epsilon = 1e-06
 F32 = jnp.float32
@@ -28,11 +32,11 @@
 
 
 def kernel(
-    acts, routes, gates, gain, gw, uw, dw, out,
-    x0, x1, xs, xs2, x3, ga, gb, gc, mt, tab_a, tab_b, tab_c,
+    acts, routes_hbm, gates_hbm, gain, gw, uw, dw, out,
+    routes, gates,    x0, x1, xs, xs2, x3, ga, gb, gc, mt, tab_a, tab_b, tab_c, mix_c,
     wg, wu, wd, ag, zs, rw, pre, acc, hid, pf, s1, s1r, s2, s2r, plain, plainr, eob, ret,
     in_sem, w_sem, wp_ssem, wp_rsem, t_ssem, t_rsem, b_ssem, b_rsem,
-    x_ssem, z_ssem, z_rsem, xl_rsem, xr_rsem, rl_rsem, rr_rsem, a_rsem, c_rsem, d_rsem, e_rsem, p_rsem, q_rsem, v_rsem, u_rsem, r_rsem,
+    x_ssem, z_ssem, z_rsem, y_rsem, xl_rsem, xr_rsem, rl_rsem, rr_rsem, a_rsem, c_rsem, d_rsem, e_rsem, p_rsem, q_rsem, v_rsem, u_rsem, r_rsem,
 ):
     p = lax.axis_index("pipe")
     q = lax.axis_index("expert")
@@ -50,7 +54,7 @@
     def other(t):
         return 1 - c if CROSS[t] else c
 
-    near = NZ - DIRECT
+    near = NZ - 1
     partner = dev(0, z, x, 1 - c)
     right = dev(0, z, lax.rem(x + 1, NX), c)
     left = dev(0, z, lax.rem(x + 3, NX), c)
@@ -89,6 +93,13 @@
 
     def home_z(t, k):
         return z_next(k) if t == 1 else z_even((0, 3, 1, 2)[k])
+
+    loads = [(routes_hbm, routes), (gates_hbm, gates), (gain.at[0], ga), (gain.at[(9 - p) // 8], gc)]
+    for i, (src, dst) in enumerate(loads[:2]):
+        pltpu.make_async_copy(src, dst, in_sem.at[i]).start()
+    each(lambda h: pltpu.make_async_copy(acts.at[0, :, cols(h)], x0.at[h], in_sem.at[4]).start())
+    for i, (src, dst) in enumerate(loads[2:]):
+        pltpu.make_async_copy(src, dst, in_sem.at[2 + i]).start()
 
     barrier = pltpu.get_barrier_semaphore()
     flows = {(dp, cross) for t, pair in enumerate(((0, 2), (7, 1), (0, 1))) for dp in pair for cross in (CROSS[t],)}
@@ -102,10 +113,8 @@
     v1 = (8 - p) // 8
     v2 = (9 - p) // 8
 
-    each(lambda h: pltpu.make_async_copy(acts.at[0, :, cols(h)], x0.at[h], in_sem.at[0]).start())
-    pltpu.make_async_copy(gain.at[0], ga, in_sem.at[1]).start()
-    pltpu.make_async_copy(gain.at[v2], gc, in_sem.at[2]).start()
     mats = ((gw, wg), (uw, wu), (dw, wd))
+
     earlier = (
         lax.broadcasted_iota(jnp.int32, (TOK, TOK), 0) < lax.broadcasted_iota(jnp.int32, (TOK, TOK), 1)
     ).astype(F32).astype(BF16)
@@ -125,6 +134,8 @@
             mt[t, e * CAP:(e + 1) * CAP] = jnp.where(here, weight[e], F32(0.0))
         return carry
 
+    for i, (src, dst) in enumerate(loads[:2]):
+        pltpu.make_async_copy(src, dst, in_sem.at[i]).wait()
     lax.fori_loop(0, TICKS, table, 0)
 
     def chosen(tab):
@@ -157,41 +168,53 @@
             for k in DORD:
                 if not (local and k == 0):
                     zz = dst_z(t, k)
-                    send(zs.at[t, zz], ag.at[t, :, 0, k], z_ssem.at[t], z_rsem.at[t, k], dev(dp, zz, x, other(t)))
+                    to = dev(dp, zz, x, other(t))
+                    if k < GATHER_NEAR[t]:
+                        send(zs.at[t, zz], ag.at[t, :, 0, k], z_ssem.at[t], z_rsem.at[t, k], to)
+                    else:
+                        for h in range(H):
+                            send(zs.at[t, zz, h], ag.at[t, h, 0, k], z_ssem.at[t], y_rsem.at[t, k - 2, h], to)
             if local:
                 for h in range(H):
                     ag[t, h, 0, 0] = zs[t, z, h]
         return go
 
-    def expert(t, sel, local, home, before_first, after_first, before_end):
+    def expert(t, sel, local, home, before_first, after_first, after_z, before_end):
         def first(k):
+            if k >= GATHER_NEAR[t]:
+                for h in range(H):
+                    got(ag.at[t, h, 0, k], y_rsem.at[t, k - 2, h])
+                    v_sem = v_rsem.at[t % 2, k - 2]
+                    send(ag.at[t, h, 0, k], ag.at[t, h, 3, k], x_ssem.at[11 if k == 3 else 13], v_sem.at[0, h], across)
+                    send(ag.at[t, h, 0, k], ag.at[t, h, 1, k], x_ssem.at[0], v_sem.at[1, h], right)
+                    send(ag.at[t, h, 0, k], ag.at[t, h, 2, k], x_ssem.at[1], v_sem.at[2, h], left)
+                return
             if not (local and k == 0):
                 got(ag.at[t, :, 0, k], z_rsem.at[t, k])
-            if k >= near:
-                send(ag.at[t, :, 0, k], ag.at[t, :, 3, k], x_ssem.at[11], v_rsem.at[t % 2, k], across)
             send(ag.at[t, :, 0, k], ag.at[t, :, 1, k], x_ssem.at[0], xl_rsem.at[t % 2, k], right)
             send(ag.at[t, :, 0, k], ag.at[t, :, 2, k], x_ssem.at[1], xr_rsem.at[t % 2, k], left)
 
         def relay(k):
             got(ag.at[t, :, 1, k], xl_rsem.at[t % 2, k])
-            if k < near:
-                send(ag.at[t, 0, 1, k], ag.at[t, 0, 3, k], x_ssem.at[2], rl_rsem.at[t % 2], right)
+            send(ag.at[t, 0, 1, k], ag.at[t, 0, 3, k], x_ssem.at[2 if k < 2 else 14], rl_rsem.at[t % 2], right)
             got(ag.at[t, :, 2, k], xr_rsem.at[t % 2, k])
-            if k < near:
-                send(ag.at[t, 1, 2, k], ag.at[t, 1, 3, k], x_ssem.at[3], rr_rsem.at[t % 2], left)
-            else:
-                got(ag.at[t, :, 3, k], v_rsem.at[t % 2, k])
+            send(ag.at[t, 1, 2, k], ag.at[t, 1, 3, k], x_ssem.at[3 if k < 2 else 15], rr_rsem.at[t % 2], left)
 
         before_first()
         first(0)
         after_first()
         first(1)
         first(2)
-        relay(0)
-        first(3)
+        if t == 1:
+            first(3)
+            relay(0)
+        else:
+            relay(0)
+            first(3)
+        after_z()
         relay(1)
-        relay(2)
-        relay(3)
+        if GATHER_NEAR[t] > 2:
+            relay(2)
 
         if t == 0:
             for i, (src, dst) in enumerate(mats[:2]):
@@ -205,8 +228,10 @@
                     got(dst.at[1, 1 - c], wp_rsem.at[1, i])
 
         for h in range(H):
-            if near:
-                got(ag.at[t, h, 3, 0:near], (rl_rsem if h == 0 else rr_rsem).at[t % 2])
+            got(ag.at[t, h, 3, 0:GATHER_NEAR[t]], (rl_rsem if h == 0 else rr_rsem).at[t % 2])
+            for k in range(GATHER_NEAR[t], NZ):
+                for i, slot in enumerate((3, 1, 2)):
+                    got(ag.at[t, h, slot, k], v_rsem.at[t % 2, k - 2, i, h])
             rows = ag[t, h].astype(F32).reshape(TOK, DH).astype(BF16)
             at = pl.ds(h * DH, DH)
             for i in range(2):
@@ -234,12 +259,19 @@
                 s2[t, h, k] = part[2 - h, k].astype(BF16)
             ahead, behind = (right, left) if h == 0 else (left, right)
             d_sem, p_sem = (d_rsem, p_rsem) if h == 0 else (e_rsem, q_rsem)
+            a_sem = a_rsem if h == 0 else c_rsem
+
+            def shared(k):
+                send(s1.at[t, h, k], s1r.at[t, h, k], x_ssem.at[4 + h], a_sem.at[t % 2, k], ahead)
+
+            for k in reversed(range(near - EARLY, near)):
+                shared(k)
             for k in reversed(range(near, NZ)):
-                send(s1.at[t, h, k], s1r.at[t, h, k], x_ssem.at[12], u_rsem.at[t % 2, h, k], across)
+                send(s1.at[t, h, k], s1r.at[t, h, k], x_ssem.at[12], u_rsem.at[t % 2, h, k - near], across)
                 send(s2.at[t, h, k], s2r.at[t, h, k], x_ssem.at[6 + h], d_sem.at[t % 2, k], ahead)
-                send(plain.at[t, h, k], plainr.at[t, h, k], x_ssem.at[9 + h], p_sem.at[t % 2, k], behind)
-            for k in reversed(range(near)):
-                send(s1.at[t, h, k], s1r.at[t, h, k], x_ssem.at[4 + h], (a_rsem if h == 0 else c_rsem).at[t % 2, k], ahead)
+                send(plain.at[t, h, k], plainr.at[t, h, k], x_ssem.at[9 + h], p_sem.at[t % 2, 1 + k - near], behind)
+            for k in reversed(range(near - EARLY)):
+                shared(k)
         if near:
             at = slice(0, near)
             send(plain.at[t, 1, at], plainr.at[t, 1, at], x_ssem.at[10], q_rsem.at[t % 2, 0], right)
@@ -254,23 +286,30 @@
             send(s2.at[t, 1, k], s2r.at[t, 1, k], x_ssem.at[7], e_rsem.at[t % 2, k], left)
 
         def final(k):
-            if k >= near:
-                for h in range(H):
-                    got(s1r.at[t, h, k], u_rsem.at[t % 2, h, k])
-                    got(plainr.at[t, h, k], (p_rsem if h == 0 else q_rsem).at[t % 2, k])
-            got(s2r.at[t, 0, k], d_rsem.at[t % 2, k])
-            got(s2r.at[t, 1, k], e_rsem.at[t % 2, k])
+            to = dev(home, home_z(t, k), x, other(t))
+            if k < near:
+                got(s2r.at[t, 0, k], d_rsem.at[t % 2, k])
+                got(s2r.at[t, 1, k], e_rsem.at[t % 2, k])
             for h in range(H):
+                if k >= near:
+                    got(s1r.at[t, h, k], u_rsem.at[t % 2, h, k - near])
+                    got(plainr.at[t, h, k], (p_rsem if h == 0 else q_rsem).at[t % 2, 1 + k - near])
+                    got(s2r.at[t, h, k], (d_rsem if h == 0 else e_rsem).at[t % 2, k])
                 total = pf[h, 0, k] + s2r[t, h, k].astype(F32) + plainr[t, h, k].astype(F32)
                 if k >= near:
                     total += s1r[t, h, k].astype(F32)
                 eob[t, k, h] = total.astype(BF16)
-            send(eob.at[t, k], ret.at[t, z], x_ssem.at[8], r_rsem.at[t], dev(home, home_z(t, k), x, other(t)))
-
-        for k in reversed(range(near)):
+                if k >= near:
+                    send(eob.at[t, k, h], ret.at[t, z, h], x_ssem.at[8], r_rsem.at[t], to)
+            if k < near:
+                send(eob.at[t, k], ret.at[t, z], x_ssem.at[8], r_rsem.at[t], to)
+
+        for k in reversed(range(MID, near)):
             middle(k)
         for k in reversed(range(near, NZ)):
             final(k)
+        for k in reversed(range(MID)):
+            middle(k)
         if near:
             got(plainr.at[t, 0, 0:near], p_rsem.at[t % 2, 0])
             got(plainr.at[t, 1, 0:near], q_rsem.at[t % 2, 0])
@@ -282,17 +321,17 @@
     def experts_sent():
         sent(ag.at[:, :, 0], x_ssem.at[0])
         sent(ag.at[:, :, 0], x_ssem.at[1])
-        if near:
-            sent(ag.at[:, 0, 1, 0:near], x_ssem.at[2])
-            sent(ag.at[:, 1, 2, 0:near], x_ssem.at[3])
-            sent(s1.at[:, 0, 0:near], x_ssem.at[4])
-            sent(s1.at[:, 1, 0:near], x_ssem.at[5])
-        if near < NZ:
-            sent(ag.at[:, :, 3, near:], x_ssem.at[11])
-            sent(s1.at[:, :, near:], x_ssem.at[12])
+        sent(ag.at[:, 0, 1, 0:2], x_ssem.at[2])
+        sent(ag.at[:, 1, 2, 0:2], x_ssem.at[3])
+        sent(ag.at[0, :, 3, 2], x_ssem.at[13])
+        sent(ag.at[0:2, 0, 1, 2], x_ssem.at[14])
+        sent(ag.at[0:2, 1, 2, 2], x_ssem.at[15])
+        sent(s1.at[:, 0, 0:near], x_ssem.at[4])
+        sent(s1.at[:, 1, 0:near], x_ssem.at[5])
+        sent(ag.at[:, :, 3, near:], x_ssem.at[11])
+        sent(s1.at[:, :, near:], x_ssem.at[12])
         sent(s2.at[:, 0], x_ssem.at[6])
         sent(s2.at[:, 1], x_ssem.at[7])
-        sent(eob, x_ssem.at[8])
         sent(plain.at[:, 0], x_ssem.at[9])
         sent(plain.at[:, 1], x_ssem.at[10])
 
@@ -323,9 +362,9 @@
 
         each(one)
 
-    pltpu.make_async_copy(x0, x0, in_sem.at[0]).wait()
-    pltpu.make_async_copy(gain.at[0], ga, in_sem.at[1]).wait()
-    pltpu.make_async_copy(gain.at[v2], gc, in_sem.at[2]).wait()
+    pltpu.make_async_copy(x0, x0, in_sem.at[4]).wait()
+    for i, (src, dst) in enumerate(loads[2:]):
+        pltpu.make_async_copy(src, dst, in_sem.at[2 + i]).wait()
     pick0 = chosen(mt[0])
 
     def gather(h):
@@ -337,7 +376,7 @@
     go = dispatch(0, ga, 0, True)
     pl.semaphore_wait(barrier, len(peers))
     for i, (src, dst) in enumerate(mats):
-        send(src.at[0, 0], dst.at[0, c], wp_ssem.at[0, i], wp_rsem.at[0, i], partner)
+        send(src.at[0, 0], dst.at[0, c], wp_ssem.at[i], wp_rsem.at[0, i], partner)
     go()
 
     def background():
@@ -351,7 +390,7 @@
         def _():
             for i, (src, dst) in enumerate(mats):
                 pltpu.make_async_copy(src.at[1, 0], dst.at[1, c], w_sem.at[1, i]).start()
-                send(src.at[1, 0], dst.at[1, c], wp_ssem.at[1, i], wp_rsem.at[1, i], partner)
+                send(src.at[1, 0], dst.at[1, c], wp_ssem.at[3 + i], wp_rsem.at[1, i], partner)
 
     def ready1():
         got(tab_a, t_rsem.at[0])
@@ -363,7 +402,7 @@
     def nothing():
         pass
 
-    expert(0, 0, True, 2, nothing, background, ready1)
+    expert(0, 0, True, 2, nothing, background, nothing, ready1)
 
     choose_rows(0, tab_a[...], tab_b[...])
     dispatch(1, gb, 7, False)()
@@ -376,7 +415,7 @@
 
         each(one)
 
-    expert(1, v1, False, 1, update1, nothing, lambda: prepare(mt[2], xs))
+    expert(1, v1, False, 1, update1, nothing, nothing, lambda: prepare(mt[2], xs))
 
     choose_rows(1, tab_b[...], mt[2])
     dispatch(2, gc, 0, not CROSS[2])()
@@ -386,38 +425,42 @@
 
         def one(h):
             xs2[h] = combine(1, xs, mix, h).astype(BF16)
+
+        each(one)
+        for h in range(LATE):
             send(xs2.at[h], x3.at[h], b_ssem.at[1], b_rsem.at[1], same(1))
 
-        each(one)
+    def ahead2():
+        for h in range(LATE, H):
+            send(xs2.at[h], x3.at[h], b_ssem.at[1], b_rsem.at[1], same(1))
 
     def ready3():
         got(tab_c, t_rsem.at[2])
+        mix_c[...] = mixer(tab_c[...])
         got(x3, b_rsem.at[1])
-
-    expert(2, v2, not CROSS[2], 1, nothing, update2, ready3)
-    mix_c = mixer(tab_c[...])
-
+        for t in range(TICKS):
+            n = 4 if t == 1 or CROSS[t] else 3
+            sent(zs.at[t, 0:n], z_ssem.at[t])
+        experts_sent()
+        for i, (src, dst) in enumerate(mats):
+            sent(src.at[0, 0], wp_ssem.at[i])
+        for i in range(3):
+            sent(mt.at[i], t_ssem.at[i])
+        sent(gb, t_ssem.at[3])
+        sent(x0, b_ssem.at[0])
+        sent(xs2, b_ssem.at[1])
+
+        @pl.when(p < 2)
+        def _():
+            for i, (src, dst) in enumerate(mats):
+                sent(src.at[1, 0], wp_ssem.at[3 + i])
+
+    expert(2, v2, not CROSS[2], 1, nothing, update2, ahead2, ready3)
     def finish(h):
-        out[0, :, cols(h)] = combine(2, x3, mix_c, h).astype(BF16)
+        out[0, :, cols(h)] = combine(2, x3, mix_c[...], h).astype(BF16)
 
     each(finish)
-
-    for t in range(TICKS):
-        n = 4 if t == 1 or CROSS[t] else 3
-        sent(zs.at[t, 0:n], z_ssem.at[t])
-    experts_sent()
-    for i, (src, dst) in enumerate(mats):
-        sent(src.at[0, 0], wp_ssem.at[0, i])
-    for i in range(3):
-        sent(mt.at[i], t_ssem.at[i])
-    sent(gb, t_ssem.at[3])
-    sent(x0, b_ssem.at[0])
-    sent(xs2, b_ssem.at[1])
-
-    @pl.when(p < 2)
-    def _():
-        for i, (src, dst) in enumerate(mats):
-            sent(src.at[1, 0], wp_ssem.at[1, i])
+    sent(eob, x_ssem.at[8])
 
 
 def per_device(acts, routes, gates, norm_gain, gate_weight, up_weight, down_weight):
@@ -429,9 +472,10 @@
     bulk = (H, TOK, DH)
     T = (SLOTS, TOK)
     scratch = [
+        V((TICKS, 1, TOPK, TOK), jnp.int32), V((TICKS, 1, TOPK, TOK), F32),
         V(bulk, BF16), V(bulk, BF16), V(bulk, BF16), V(bulk, BF16), V(bulk, BF16),
         V((1, D), F32), V((1, D), F32), V((1, D), F32),
-        V((TICKS, SLOTS, TOK), F32), V(T, F32), V(T, F32), V(T, F32),
+        V((TICKS, SLOTS, TOK), F32), V(T, F32), V(T, F32), V(T, F32), V((TOK, TOK), BF16),
         V((2, 2, D, HID), BF16), V((2, 2, D, HID), BF16), V((2, 2, HID, D), BF16),
         V((TICKS, H, NX, NZ, CAP, DH), BF16),
         V((TICKS, EXPERTS, H, CAP, DH), BF16),
@@ -444,14 +488,14 @@
         V((TICKS, H, NZ, CAP, DH), BF16), V((TICKS, H, NZ, CAP, DH), BF16),
         V((TICKS, NZ, H, CAP, DH), BF16),
         V((TICKS, EXPERTS, H, CAP, DH), BF16),
-        S((3,)), S((2, 3)), S((2, 3)), S((2, 3)), S((4,)), S((4,)), S((2,)), S((2,)),
+        S((5,)), S((2, 3)), S((6,)), S((2, 3)), S((4,)), S((4,)), S((2,)), S((2,)),
     ]
-    scratch += [S((13,)), S((TICKS,)), S((TICKS, NZ)), S((2, NZ)), S((2, NZ)), S((2,)), S((2,))]
-    scratch += [S((2, NZ))] * 4 + [S((2, NZ))] * 3 + [S((2, 2, NZ)), S((TICKS,))]
+    scratch += [S((16,)), S((TICKS,)), S((TICKS, 3)), S((TICKS, 2, H)), S((2, 3)), S((2, 3)), S((2,)), S((2,))]
+    scratch += [S((2, 3))] * 2 + [S((2, NZ))] * 2 + [S((2, 2))] * 2 + [S((2, 2, 3, H)), S((2, H, 1)), S((TICKS,))]
     return pl.pallas_call(
         kernel,
         out_shape=jax.ShapeDtypeStruct((1, TOK, D), BF16),
-        in_specs=[anyw, vmem, vmem, anyw, anyw, anyw, anyw],
+        in_specs=[anyw, anyw, anyw, anyw, anyw, anyw, anyw],
         out_specs=vmem,
         scratch_shapes=scratch,
         compiler_params=pltpu.CompilerParams(

time: 103 us -> 101 us (0.981)
  Pallas kernels: 102 us -> 100 us
    pallas_call x1, Pallas kernels: 102 us -> 100 us  [per_device(): pl.pallas_call(kernel, out_shape=jax.ShapeDtypeStruct((1, TOK, D), BF16),...]
where the time goes in v2:
time: 101 us
  Pallas kernels  100 us (99%)
    pallas_call x1, Pallas kernels, per_device(): pl.pallas_call(kernel, out_shape=jax.ShapeDtypeStruct((1, TOK, D), BF16),...  100 us

profile of v2, /device:TPU:32, one launch (start us, length us, event | category | flops | bytes accessed | tf_op | source)
XLA Modules:
  0.0 101.0 jit_solution(13325050710204774908)
XLA Ops:
  0.0 100.0 %shard_map.73 = bf16[1,128,3584]{2,1,0:T(8,128)(2,1)S(1)} custom-call(bf16[1,128,3584]{2,1,0:T(8,128)(2,1)} %acts.1, s32[3,1,8,128]{3,2,1,0:T(8,128)} %bitcast.2, f32[3,1,8,128]{3,2,1,0:T(8,128)} %bitcast.3, f32[2,1,3584]{2,1,0:T(1,128)} %gain.1, bf16[2,1,3584,256]{3,2,1,0:T(8,128)(2,1)} %gw.1, bf16[2,1,3584,256]{3,2,1,0:T(8,128)(2,1)} %uw.1, ...), custom_call_target="tpu_custom_call" | custom-call | tf_op jit(solution)/shard_map/pallas_call | solution.py:495
  100.0 0.9 copy.9

commit v3 on v2

--- a/solution.py
+++ b/solution.py
@@ -147,7 +147,7 @@
 
     def mixer(tab):
         high, low = halves(tab)
-        return jnp.concatenate([high, low, jnp.zeros((64, TOK), F32)], axis=0).T.astype(BF16)
+        return jnp.concatenate([high, low], axis=0).T.astype(BF16)
 
     def returned(t, h):
         return ret[t, :, h].astype(F32).reshape(SLOTS, DH)
@@ -184,10 +184,10 @@
             if k >= GATHER_NEAR[t]:
                 for h in range(H):
                     got(ag.at[t, h, 0, k], y_rsem.at[t, k - 2, h])
-                    v_sem = v_rsem.at[t % 2, k - 2]
-                    send(ag.at[t, h, 0, k], ag.at[t, h, 3, k], x_ssem.at[11 if k == 3 else 13], v_sem.at[0, h], across)
-                    send(ag.at[t, h, 0, k], ag.at[t, h, 1, k], x_ssem.at[0], v_sem.at[1, h], right)
-                    send(ag.at[t, h, 0, k], ag.at[t, h, 2, k], x_ssem.at[1], v_sem.at[2, h], left)
+                    v_sem = v_rsem.at[t % 2, k - 2, h]
+                    send(ag.at[t, h, 0, k], ag.at[t, h, 3, k], x_ssem.at[11 if k == 3 else 13], v_sem, across)
+                    send(ag.at[t, h, 0, k], ag.at[t, h, 1, k], x_ssem.at[0], v_sem, right)
+                    send(ag.at[t, h, 0, k], ag.at[t, h, 2, k], x_ssem.at[1], v_sem, left)
                 return
             if not (local and k == 0):
                 got(ag.at[t, :, 0, k], z_rsem.at[t, k])
@@ -230,8 +230,7 @@
         for h in range(H):
             got(ag.at[t, h, 3, 0:GATHER_NEAR[t]], (rl_rsem if h == 0 else rr_rsem).at[t % 2])
             for k in range(GATHER_NEAR[t], NZ):
-                for i, slot in enumerate((3, 1, 2)):
-                    got(ag.at[t, h, slot, k], v_rsem.at[t % 2, k - 2, i, h])
+                got(ag.at[t, h, 1:NX, k], v_rsem.at[t % 2, k - 2, h])
             rows = ag[t, h].astype(F32).reshape(TOK, DH).astype(BF16)
             at = pl.ds(h * DH, DH)
             for i in range(2):
@@ -337,7 +336,7 @@
 
     def combine(t, xref, mix, h):
         rows = returned(t, h)
-        rows = jnp.concatenate([rows, rows, jnp.zeros((64, DH), F32)], axis=0).astype(BF16)
+        rows = jnp.concatenate([rows, rows], axis=0).astype(BF16)
         return xref[h].astype(F32) + jnp.dot(mix, rows, preferred_element_type=F32)
 
     def prepare(tab, xref):
@@ -475,7 +474,7 @@
         V((TICKS, 1, TOPK, TOK), jnp.int32), V((TICKS, 1, TOPK, TOK), F32),
         V(bulk, BF16), V(bulk, BF16), V(bulk, BF16), V(bulk, BF16), V(bulk, BF16),
         V((1, D), F32), V((1, D), F32), V((1, D), F32),
-        V((TICKS, SLOTS, TOK), F32), V(T, F32), V(T, F32), V(T, F32), V((TOK, TOK), BF16),
+        V((TICKS, SLOTS, TOK), F32), V(T, F32), V(T, F32), V(T, F32), V((TOK, 2 * SLOTS), BF16),
         V((2, 2, D, HID), BF16), V((2, 2, D, HID), BF16), V((2, 2, HID, D), BF16),
         V((TICKS, H, NX, NZ, CAP, DH), BF16),
         V((TICKS, EXPERTS, H, CAP, DH), BF16),
@@ -491,7 +490,7 @@
         S((5,)), S((2, 3)), S((6,)), S((2, 3)), S((4,)), S((4,)), S((2,)), S((2,)),
     ]
     scratch += [S((16,)), S((TICKS,)), S((TICKS, 3)), S((TICKS, 2, H)), S((2, 3)), S((2, 3)), S((2,)), S((2,))]
-    scratch += [S((2, 3))] * 2 + [S((2, NZ))] * 2 + [S((2, 2))] * 2 + [S((2, 2, 3, H)), S((2, H, 1)), S((TICKS,))]
+    scratch += [S((2, 3))] * 2 + [S((2, NZ))] * 2 + [S((2, 2))] * 2 + [S((2, 2, H)), S((2, H, 1)), S((TICKS,))]
     return pl.pallas_call(
         kernel,
         out_shape=jax.ShapeDtypeStruct((1, TOK, D), BF16),

time: 101 us -> 101 us (level)
  no operation moved by 1% of the time
where the time goes in v3:
time: 101 us
  Pallas kernels  100 us (99%)
    pallas_call x1, Pallas kernels, per_device(): pl.pallas_call(kernel, out_shape=jax.ShapeDtypeStruct((1, TOK, D), BF16),...  100 us

profile of v3, /device:TPU:32, one launch (start us, length us, event | category | flops | bytes accessed | tf_op | source)
XLA Modules:
  0.0 101.0 jit_solution(4869364068638719150)
XLA Ops:
  0.0 100.1 %shard_map.73 = bf16[1,128,3584]{2,1,0:T(8,128)(2,1)S(1)} custom-call(bf16[1,128,3584]{2,1,0:T(8,128)(2,1)} %acts.1, s32[3,1,8,128]{3,2,1,0:T(8,128)} %bitcast.2, f32[3,1,8,128]{3,2,1,0:T(8,128)} %bitcast.3, f32[2,1,3584]{2,1,0:T(1,128)} %gain.1, bf16[2,1,3584,256]{3,2,1,0:T(8,128)(2,1)} %gw.1, bf16[2,1,3584,256]{3,2,1,0:T(8,128)(2,1)} %uw.1, ...), custom_call_target="tpu_custom_call" | custom-call | tf_op jit(solution)/shard_map/pallas_call | solution.py:494
  100.1 0.9 copy.9
